TPU v7x, 32 devices: a whole 2x2x4 slice. The times are simulated.
32 devices in a mesh: gy: 16 (over z, y, core), gz: 2 (over x).
Axes of the slice: x: 2, y: 2, z: 4, core: 2. Of those that a mesh axis runs over, the one named last changes fastest.
Arguments:
- omega: float32 [3, 256, 128, 128], P(None, 'gy', 'gz'), may hold values from -6 to 6
- velocity: float32 [3, 256, 128, 128], P(None, 'gy', 'gz'), may hold values from -6 to 6
- point_owner: int32 [1152], replicated, may hold values from 0 to 22, as said below
- point_cells: int32 [3, 1152], replicated, may hold values from 1 to 125, as said below
- point_frac: float32 [3, 1152], replicated, may hold values from 0 to 1
- chord: float32 [1152], replicated, may hold values from 0.2 to 1
- twist: float32 [1152], replicated, may hold values from -0.3 to 0.3
- angle_step: int32 [1], replicated, may hold values from 0 to 719
Outputs:
- omega_out: float32 [3, 256, 128, 128], P(None, 'gy', 'gz')
- blade_sources: float32 [3, 1152], replicated
Inputs may be any that keep to these rules, and one draw needn't show every extreme that they name: `point_owner`: turbine t's points lie in spanwise blocks t * 2 to (t + 1) * 2 - 1 and in the 1 vertical blocks from (1) // 2 on; no block holds more than 192 points, and in every turbine one block holds exactly 192. `point_cells`: streamwise cells lie in 1 to 125, spanwise in 1 to 13, vertical in 1 to 61; all points of a turbine share one streamwise cell.
All inputs are finite; a program needn't handle non-finite values.
Results may differ from a plain program's by a relative error of at most 0.0003.
Values sent between devices are 32-bit elements; how exact they have to be, the bound alone decides.
A program may use at most 128 MiB of HBM per device.

v0:
```python
import jax
import jax.numpy as jnp
from jax import lax
from jax.sharding import PartitionSpec as P

TURBINES = 6
BLADES = 3
BP = 64
section_step = 0.4
viscosity = 0.05
tip_speed = 3.0
turn_step = 2.0 * 3.141592653589793 / 720.0


def with_halo(x, sides, width):
    for axis, dim in sides:
        size, length = (lax.axis_size(axis), x.shape[dim])
        up = [(i, (i + 1) % size) for i in range(size - 1)]
        down = [(j, i) for i, j in up]
        last = lax.slice_in_dim(x, length - width, length, axis=dim)
        initial = lax.slice_in_dim(x, 0, width, axis=dim)
        before = lax.ppermute(last, axis, up)
        after = lax.ppermute(initial, axis, down)
        x = jnp.concatenate([before, x, after], axis=dim)
    return x


def remesh_kernel(shift):
    mag = jnp.abs(shift)
    inner = 1.0 - 2.5 * mag * mag + 1.5 * mag * mag * mag
    outer = 0.5 * (2.0 - mag) * (2.0 - mag) * (1.0 - mag)
    return jnp.where(mag < 1.0, inner, jnp.where(mag < 2.0, outer, 0.0))


def shifted(padded, axis, offset):
    index = []
    for dim in range(4):
        if dim == 0:
            index.append(slice(None))
        elif dim == axis:
            index.append(slice(offset, offset + padded.shape[dim] - 4))
        else:
            index.append(slice(2, padded.shape[dim] - 2))
    return padded[tuple(index)]


def centered_first(padded, axis):
    return (
        shifted(padded, axis, 0)
        - 8.0 * shifted(padded, axis, 1)
        + 8.0 * shifted(padded, axis, 3)
        - shifted(padded, axis, 4)
    ) / 12.0


def centered_second(padded, axis):
    return (
        -shifted(padded, axis, 0)
        + 16.0 * shifted(padded, axis, 1)
        - 30.0 * shifted(padded, axis, 2)
        + 16.0 * shifted(padded, axis, 3)
        - shifted(padded, axis, 4)
    ) / 12.0


def remesh_padded(field, displace, axis):
    length = field.shape[axis] - 4
    total = jnp.zeros(field.shape[:axis] + (length,) + field.shape[axis + 1 :], jnp.float32)
    for offset in range(-2, 3):
        start = 2 - offset
        part = lax.slice_in_dim(field, start, start + length, axis=axis)
        moved = lax.slice_in_dim(displace, start, start + length, axis=axis - 1)
        total = total + remesh_kernel(offset - moved)[None] * part
    return total


def blade_forces(point_velocity, chord, twist, angle_step):
    count = point_velocity.shape[1]
    points = jnp.arange(count, dtype=jnp.int32)
    station = points % BP
    blade = points // BP % BLADES
    theta = angle_step[0].astype(
        jnp.float32
    ) * turn_step + 2.0 * 3.141592653589793 / 3.0 * blade.astype(jnp.float32)
    radius = (station.astype(jnp.float32) + 0.5) / BP
    cos_t = jnp.cos(theta)
    sin_t = jnp.sin(theta)
    rel_x = point_velocity[0]
    rel_y = point_velocity[1] + tip_speed * radius * sin_t
    rel_z = point_velocity[2] - tip_speed * radius * cos_t
    rel_t = -sin_t * rel_y + cos_t * rel_z
    speed = jnp.sqrt(rel_x * rel_x + rel_t * rel_t + 1.0)
    gamma = 3.141592653589793 * chord * (rel_x * jnp.cos(twist) + rel_t * jnp.sin(twist))
    blades = gamma.reshape(-1, BP)
    before = jnp.concatenate([jnp.zeros((blades.shape[0], 1), jnp.float32), blades[:, :-1]], axis=1)
    shed = (blades - before).reshape(-1)
    return jnp.stack(
        [
            shed * rel_x / speed,
            gamma * cos_t + shed * rel_y / speed,
            gamma * sin_t + shed * rel_z / speed,
        ]
    )


def point_tables(
    cells,
    fracs,
    owner_span,
    owner_vert,
    span_index,
    vert_index,
    span_cells,
    vert_cells,
    axial_cells,
):
    rows_x = jnp.arange(axial_cells, dtype=jnp.int32)
    rows_y = jnp.arange(span_cells, dtype=jnp.int32)
    rows_z = jnp.arange(vert_cells, dtype=jnp.int32)
    gap_x = rows_x[:, None] - cells[0][None, :]
    gap_y = (
        span_index * span_cells
        + rows_y[:, None]
        - owner_span[None, :] * span_cells
        - cells[1][None, :]
    )
    gap_z = (
        vert_index * vert_cells
        + rows_z[:, None]
        - owner_vert[None, :] * vert_cells
        - cells[2][None, :]
    )
    table_x = remesh_kernel(gap_x.astype(jnp.float32) - fracs[0][None, :])
    table_y = remesh_kernel(gap_y.astype(jnp.float32) - fracs[1][None, :])
    table_z = remesh_kernel(gap_z.astype(jnp.float32) - fracs[2][None, :])
    return (table_x, table_y, table_z)


def on_device(omega, velocity, point_owner, point_cells, point_frac, chord, twist, angle_step):
    span_cells, vert_cells, axial_cells = (omega.shape[1], omega.shape[2], omega.shape[3])
    span_count = lax.axis_size("gy")
    vert_count = lax.axis_size("gz")
    span_index = lax.axis_index("gy")
    vert_index = lax.axis_index("gz")
    owner_span = point_owner // vert_count
    owner_vert = point_owner % vert_count
    highest = lax.Precision.HIGHEST
    busiest = 2 * (BLADES * BP) // (span_count // TURBINES * max(vert_count // 2, 1))
    my_block = span_index * vert_count + vert_index
    points = jnp.arange(point_owner.shape[0], dtype=jnp.int32)
    ranking = jnp.where(point_owner == my_block, points, points + point_owner.shape[0])
    picked = jnp.argsort(ranking, stable=True)[:busiest]
    selector = (picked[:, None] == points[None, :]).astype(jnp.float32)
    table_x, table_y, table_z = point_tables(
        point_cells[:, picked],
        point_frac[:, picked],
        owner_span[picked],
        owner_vert[picked],
        span_index,
        vert_index,
        span_cells,
        vert_cells,
        axial_cells,
    )
    columns = jnp.dot(
        velocity.reshape(-1, axial_cells),
        table_x,
        precision=highest,
        preferred_element_type=jnp.float32,
    )
    columns = columns.reshape(3, span_cells, vert_cells, -1)
    compact = jnp.einsum("cyzq,yq,zq->cq", columns, table_y, table_z, precision=highest)
    partial_velocity = jnp.dot(
        compact, selector, precision=highest, preferred_element_type=jnp.float32
    )
    point_velocity = lax.psum(partial_velocity, ("gy", "gz"))
    sources = blade_forces(point_velocity, chord, twist, angle_step)
    local_sources = sources[:, picked]
    spread = jnp.einsum("cq,yq,zq->cyzq", local_sources, table_y, table_z, precision=highest)
    smear = jnp.dot(
        spread.reshape(-1, spread.shape[3]),
        table_x.T,
        precision=highest,
        preferred_element_type=jnp.float32,
    )
    smear = smear.reshape(3, span_cells, vert_cells, axial_cells)
    omega_rim, velocity_rim = (
        with_halo(omega, (("gy", 1), ("gz", 2)), 2),
        with_halo(velocity, (("gy", 1), ("gz", 2)), 2),
    )
    axial_pads = ((0, 0), (0, 0), (0, 0), (2, 2))
    omega_pad = jnp.pad(omega_rim, axial_pads)
    velocity_pad = jnp.pad(velocity_rim, axial_pads)
    stretch = jnp.zeros_like(omega)
    laplace = jnp.zeros_like(omega)
    for axis in range(3):
        stretch = stretch + omega[2 - axis][None] * centered_first(velocity_pad, 3 - axis)
        laplace = laplace + centered_second(omega_pad, axis + 1)
    section = omega + section_step * (stretch + viscosity * laplace + smear)
    shift_x = jnp.clip(section_step * velocity[0], -1.0, 1.0)
    moved_x = remesh_padded(
        jnp.pad(section, axial_pads), jnp.pad(shift_x, ((0, 0), (0, 0), (2, 2))), 3
    )
    shift_z = jnp.clip(section_step * velocity_rim[2][2 : span_cells + 2, :, :], -1.0, 1.0)
    span_rim = with_halo(moved_x, (("gy", 1),), 2)
    shift_y = jnp.clip(section_step * velocity_rim[1][:, 2 : vert_cells + 2, :], -1.0, 1.0)
    moved_mid = remesh_padded(span_rim, shift_y, 1)
    moved_y = with_halo(moved_mid, (("gz", 2),), 2)
    omega_out = remesh_padded(moved_y, shift_z, 2)
    return (omega_out, sources)


def solution(mesh):
    in_specs = (P(None, "gy", "gz", None), P(None, "gy", "gz", None), P(), P(), P(), P(), P(), P())
    out_specs = (P(None, "gy", "gz", None), P())
    return jax.shard_map(
        on_device, mesh=mesh, in_specs=in_specs, out_specs=out_specs, check_vma=False
    )
```

profile of v0, /device:TPU:10, one launch (start us, length us, event | category | flops | bytes accessed | tf_op | source)
XLA Modules:
  0.0 163.6 jit_solution(6236119518289551892)
XLA Ops:
  0.6 1.8 %fusion.252 = (f32[3,2,64,128]{3,2,1,0:T(8,128)}, f32[3,2,64,128]{3,2,1,0:T(8,128)}) fusion(f32[3,16,64,128]{3,2,1,0:T(8,128)} %param.9), kind=kLoop, calls=%fused_computation.439 | loop fusion | bytes 786432 | tf_op jit(solution)/shard_map/slice | solution.py:21
  2.5 2.0 %collective-permute-start = (f32[3,2,64,128]{3,2,1,0:T(8,128)}, f32[3,2,64,128]{3,2,1,0:T(8,128)}, u32[]{:S(2)}, u32[]{:S(2)}) collective-permute-start(f32[3,2,64,128]{3,2,1,0:T(8,128)} %get-tuple-element.33), channel_id=1, source_target_pairs={{0,2},{2,4},{4,6},{6,8},{8,10},{10,12},{12,14},{14,16},{16,18},{18... | collective-permute-start | bytes 589832 | tf_op jit(solution)/shard_map/ppermute | solution.py:22
  4.5 4.5 %collective-permute-start.1 = (f32[3,2,64,128]{3,2,1,0:T(8,128)}, f32[3,2,64,128]{3,2,1,0:T(8,128)}, u32[]{:S(2)}, u32[]{:S(2)}) collective-permute-start(f32[3,2,64,128]{3,2,1,0:T(8,128)} %get-tuple-element.32), channel_id=1, source_target_pairs={{2,0},{4,2},{6,4},{8,6},{10,8},{12,10},{14,12},{16,14},{18,16},{20... | collective-permute-start | bytes 589832 | tf_op jit(solution)/shard_map/ppermute | solution.py:23
  9.1 1.7 %fusion.253 = (f32[3,2,64,128]{3,2,1,0:T(8,128)S(1)}, f32[3,2,64,128]{3,2,1,0:T(8,128)}) fusion(f32[3,16,64,128]{3,2,1,0:T(8,128)} %param.8), kind=kLoop, calls=%fused_computation.440 | loop fusion | bytes 786432 | tf_op jit(solution)/shard_map/slice | solution.py:21
  10.8 2.0 %collective-permute-start.4 = (f32[3,2,64,128]{3,2,1,0:T(8,128)}, f32[3,2,64,128]{3,2,1,0:T(8,128)}, u32[]{:S(2)}, u32[]{:S(2)}) collective-permute-start(f32[3,2,64,128]{3,2,1,0:T(8,128)} %get-tuple-element.35), channel_id=1, source_target_pairs={{0,2},{2,4},{4,6},{6,8},{8,10},{10,12},{12,14},{14,16},{16,18},{18... | collective-permute-start | bytes 589832 | tf_op jit(solution)/shard_map/ppermute | solution.py:22
  12.8 4.5 %collective-permute-start.5 = (f32[3,2,64,128]{3,2,1,0:T(8,128)S(1)}, f32[3,2,64,128]{3,2,1,0:T(8,128)}, u32[]{:S(2)}, u32[]{:S(2)}) collective-permute-start(f32[3,2,64,128]{3,2,1,0:T(8,128)S(1)} %get-tuple-element.34), channel_id=1, source_target_pairs={{2,0},{4,2},{6,4},{8,6},{10,8},{12,10},{14,12},{16,14},{18,16},{20... | collective-permute-start | bytes 589832 | tf_op jit(solution)/shard_map/ppermute | solution.py:23
  17.4 5.0 %sort.17 = (s32[1152]{0:T(1024)}, s32[1152]{0:T(1024)S(1)}) sort(s32[1152]{0:T(1024)S(1)} %get-tuple-element.63, s32[1152]{0:T(1024)S(1)} %iota.43), dimensions={0}, to_apply=%region_0.1 | sort | flops 12672 | bytes 18432 | tf_op jit(solution)/shard_map/jit(argsort)/sort | solution.py:152
  22.5 1.4 gather_fusion.3
  27.0 3.6 %convolution_bitcast_fusion = f32[3072,192]{0,1:T(8,128)} fusion(f32[3072,128]{1,0:T(8,128)S(1)} %bitcast.49, f32[192]{0:T(256)S(1)} %get-tuple-element.8, s32[192]{0:T(256)S(1)} %get-tuple-element.5), kind=kOutput, calls=%fused_computation.18 | convolution fusion | flops 906461184 | bytes 3933696 | tf_op jit(solution)/shard_map/dot_general | solution.py:165
  30.6 2.2 %copy.29 = f32[3072,192]{1,0:T(8,128)S(1)} copy(f32[3072,192]{0,1:T(8,128)} %convolution_bitcast_fusion) | data formatting | bytes 4718592
  33.7 1.4 gather_fusion
  35.3 1.4 fusion.255
  37.2 40.4 %psum.7 = f32[3,1152]{1,0:T(4,128)S(1)} all-reduce(f32[3,1152]{1,0:T(4,128)S(1)} %fusion.77), channel_id=1, replica_groups=mesh['gy'=16,'gz'=2] {'gy','gz'}, use_global_device_ids=true, to_apply=%region_1.2 | all-reduce | flops 3456 | bytes 27648 | tf_op jit(solution)/shard_map/psum | solution.py:176
  80.7 1.3 fusion.104
  83.4 1.7 %gather_fusion.4 = f32[192,3]{1,0:T(8,128)S(1)} fusion(f32[3,1152]{0,1:T(8,128)} %copy.17, s32[1024]{0:T(1024)S(1)} %pad_clamp_fusion), kind=kCustom, calls=%fused_computation.4 | custom fusion | bytes 5376 | tf_op jit(solution)/shard_map/gather | solution.py:178
  85.3 4.3 %fusion.93 = (f32[16,64,128]{2,1,0:T(8,128)}, f32[16,64,128]{2,1,0:T(8,128)}, f32[16,64,128]{2,1,0:T(8,128)}, f32[16,64,128]{2,1,0:T(8,128)}) fusion(f32[16,64,128]{2,1,0:T(8,128)} %get-tuple-element.22), kind=kLoop, calls=%fused_computation.199 | loop fusion | flops 9437184 | bytes 2621440 | tf_op jit(solution)/shard_map/jit(_where)/select_n | solution.py:32
  94.4 4.7 %collective-permute-start.3 = (f32[3,20,2,128]{3,2,1,0:T(2,128)S(1)}, f32[3,20,2,128]{3,2,1,0:T(2,128)S(1)}, u32[]{:S(2)}, u32[]{:S(2)}) collective-permute-start(f32[3,20,2,128]{3,2,1,0:T(2,128)S(1)} %get-tuple-element.14), channel_id=1, source_target_pairs={{1,0},{3,2},{5,4},{7,6},{9,8},{11,10},{13,12},{15,14},{17,16},{19,... | collective-permute-start | bytes 184328 | tf_op jit(solution)/shard_map/ppermute | solution.py:23
  102.0 1.3 collective-permute-start.6
  103.3 4.5 %collective-permute-start.7 = (f32[3,20,2,128]{3,2,1,0:T(2,128)S(1)}, f32[3,20,2,128]{3,2,1,0:T(2,128)S(1)}, u32[]{:S(2)}, u32[]{:S(2)}) collective-permute-start(f32[3,20,2,128]{3,2,1,0:T(2,128)S(1)} %get-tuple-element.16), channel_id=1, source_target_pairs={{1,0},{3,2},{5,4},{7,6},{9,8},{11,10},{13,12},{15,14},{17,16},{19,... | collective-permute-start | bytes 184328 | tf_op jit(solution)/shard_map/ppermute | solution.py:23
  107.9 1.7 %pad_maximum_fusion = f32[3,20,68,128]{3,2,1,0:T(8,128)} fusion(f32[3,20,2,128]{3,2,1,0:T(2,128)S(1)} %collective-permute-done.3, f32[3,20,64,128]{3,2,1,0:T(8,128)S(1)} %get-tuple-element.53, f32[3,20,2,128]{3,2,1,0:T(2,128)S(1)} %collective-permute-done.2), kind=kLoop, calls=%fused_computation.23 | loop fusion | flops 1044480 | bytes 4177920 | tf_op jit(solution)/shard_map/concatenate | solution.py:24
  110.8 3.5 %select_maximum_fusion = f32[3,20,68,132]{3,2,1,0:T(8,128)} fusion(f32[3,20,2,128]{3,2,1,0:T(2,128)S(1)} %collective-permute-done.7, f32[3,20,64,128]{3,2,1,0:T(8,128)S(1)} %get-tuple-element.57, f32[3,20,2,128]{3,2,1,0:T(2,128)S(1)} %collective-permute-done.6), kind=kLoop, calls=%fused_computation.15 | loop fusion | flops 4308480 | bytes 4243200 | tf_op jit(solution)/shard_map/concatenate | solution.py:24
  114.4 20.4 %fusion.30 = f32[3,16,64,128]{3,2,1,0:T(8,128)} fusion(f32[3,16,64,128]{3,2,1,0:T(8,128)S(1)} %copy-done.2, f32[3,20,64,128]{3,2,1,0:T(8,128)} %copy-done.4, f32[3,20,2,128]{3,2,1,0:T(2,128)S(1)} %collective-permute-done.7, f32[3,20,2,128]{3,2,1,0:T(2,128)S(1)} %collective-permute-done.6, f32[3,20,64,128]{3,2,1,0:T(8,128)} %copy-done.3, ...), kind=kOutput, calls=%fused_computation.70 | convolution fusion | flops 929464320 | bytes 29947392 | tf_op jit(solution)/shard_map/dot_general | solution.py:180
  134.7 6.4 %fusion.48 = f32[3,16,64,128]{3,2,1,0:T(8,128)S(1)} fusion(f32[3,16,64,128]{3,2,1,0:T(8,128)} %fusion.30, f32[16,64,128]{2,1,0:T(8,128)} %get-tuple-element.49, f32[16,64,128]{2,1,0:T(8,128)} %get-tuple-element.48, f32[16,64,128]{2,1,0:T(8,128)S(1)} %copy-done.5, f32[16,64,128]{2,1,0:T(8,128)} %get-tuple-element.47, f32[16,64,128]{2,1,0:T(8,128)} %get-tuple-element.46), kind=kLoop, calls=%fused_computation.88 | loop fusion | flops 3538944 | bytes 5767168 | tf_op jit(solution)/shard_map/add | solution.py:73
  141.2 1.9 %collective-permute-start.8 = (f32[3,2,64,128]{3,2,1,0:T(8,128)S(1)}, f32[3,2,64,128]{3,2,1,0:T(8,128)S(1)}, u32[]{:S(2)}, u32[]{:S(2)}) collective-permute-start(f32[3,2,64,128]{3,2,1,0:T(8,128)S(1)} %get-tuple-element.19), channel_id=1, source_target_pairs={{2,0},{4,2},{6,4},{8,6},{10,8},{12,10},{14,12},{16,14},{18,16},{20... | collective-permute-start | bytes 589832 | tf_op jit(solution)/shard_map/ppermute | solution.py:23
  143.1 2.4 %collective-permute-start.9 = (f32[3,2,64,128]{3,2,1,0:T(8,128)S(1)}, f32[3,2,64,128]{3,2,1,0:T(8,128)S(1)}, u32[]{:S(2)}, u32[]{:S(2)}) collective-permute-start(f32[3,2,64,128]{3,2,1,0:T(8,128)S(1)} %get-tuple-element.20), channel_id=1, source_target_pairs={{0,2},{2,4},{4,6},{6,8},{8,10},{10,12},{12,14},{14,16},{16,18},{18... | collective-permute-start | bytes 589832 | tf_op jit(solution)/shard_map/ppermute | solution.py:22
  145.6 1.5 fusion.88
  148.3 2.7 %collective-permute-done.9 = f32[3,2,64,128]{3,2,1,0:T(8,128)S(1)} collective-permute-done((f32[3,2,64,128]{3,2,1,0:T(8,128)S(1)}, f32[3,2,64,128]{3,2,1,0:T(8,128)S(1)}, u32[]{:S(2)}, u32[]{:S(2)}) %collective-permute-start.9) | collective-permute-done | bytes 196640 | tf_op jit(solution)/shard_map/ppermute | solution.py:22
  151.0 1.3 fusion.15
  152.4 3.1 %collective-permute-start.10 = (f32[3,16,2,128]{3,2,1,0:T(2,128)S(1)}, f32[3,16,2,128]{3,2,1,0:T(2,128)S(1)}, u32[]{:S(2)}, u32[]{:S(2)}) collective-permute-start(f32[3,16,2,128]{3,2,1,0:T(2,128)S(1)} %get-tuple-element.17), channel_id=1, source_target_pairs={{1,0},{3,2},{5,4},{7,6},{9,8},{11,10},{13,12},{15,14},{17,16},{19,... | collective-permute-start | bytes 147464 | tf_op jit(solution)/shard_map/ppermute | solution.py:23
  156.8 1.7 %fusion.83 = (f32[16,64,128]{2,1,0:T(8,128)S(1)}, f32[16,64,128]{2,1,0:T(8,128)S(1)}, f32[16,64,128]{2,1,0:T(8,128)S(1)}, f32[16,64,128]{2,1,0:T(8,128)S(1)}, f32[16,64,128]{2,1,0:T(8,128)S(1)}) fusion(f32[16,68,128]{2,1,0:T(8,128)S(1)} %fusion.80), kind=kLoop, calls=%fused_computation.189 | loop fusion | flops 11796480 | bytes 5242880 | tf_op jit(solution)/shard_map/jit(_where)/select_n | solution.py:32
  158.5 3.0 %collective-permute-done.11 = f32[3,16,2,128]{3,2,1,0:T(2,128)S(1)} collective-permute-done((f32[3,16,2,128]{3,2,1,0:T(2,128)S(1)}, f32[3,16,2,128]{3,2,1,0:T(2,128)S(1)}, u32[]{:S(2)}, u32[]{:S(2)}) %collective-permute-start.11) | collective-permute-done | bytes 49184 | tf_op jit(solution)/shard_map/ppermute | solution.py:22
  161.5 2.1 %fusion.7 = f32[3,16,64,128]{3,2,1,0:T(8,128)} fusion(f32[3,16,2,128]{3,2,1,0:T(2,128)S(1)} %collective-permute-done.11, f32[3,16,64,128]{3,2,1,0:T(8,128)S(1)} %fusion.15, f32[3,16,2,128]{3,2,1,0:T(2,128)S(1)} %collective-permute-done.10, f32[16,64,128]{2,1,0:T(8,128)S(1)} %get-tuple-element.42, f32[16,64,128]{2,1,0:T(8,128)S(1)} %get-tuple-element.43, ...), kind=kLoop, calls=%fused_computation.47 | loop fusion | flops 5111808 | bytes 5865472 | tf_op jit(solution)/shard_map/add | solution.py:73
  (102 shorter events, 19.6 us)
Async XLA Ops:
  0.6 16.8 %copy-start.16 = (s32[1152]{0:T(1024)S(1)}, s32[1152]{0:T(1024)}, u32[]{:S(2)}) copy-start(s32[1152]{0:T(1024)} %param.10) | copy-start | bytes 13828
  0.6 23.3 %copy-start.12 = (s32[3,1152]{1,0:T(4,128)S(1)}, s32[3,1152]{1,0:T(4,128)}, u32[]{:S(2)}) copy-start(s32[3,1152]{1,0:T(4,128)} %param.11) | copy-start | bytes 41476
  2.5 22.8 %copy-start.13 = (f32[3,1152]{1,0:T(4,128)S(1)}, f32[3,1152]{1,0:T(4,128)}, u32[]{:S(2)}) copy-start(f32[3,1152]{1,0:T(4,128)} %param.12) | copy-start | bytes 41476
  2.5 87.8 %collective-permute-start = (f32[3,2,64,128]{3,2,1,0:T(8,128)}, f32[3,2,64,128]{3,2,1,0:T(8,128)}, u32[]{:S(2)}, u32[]{:S(2)}) collective-permute-start(f32[3,2,64,128]{3,2,1,0:T(8,128)} %get-tuple-element.33), channel_id=1, source_target_pairs={{0,2},{2,4},{4,6},{6,8},{8,10},{10,12},{12,14},{14,16},{16,18},{18... | collective-permute-start | bytes 589832 | tf_op jit(solution)/shard_map/ppermute | solution.py:22
  4.5 87.3 %collective-permute-start.1 = (f32[3,2,64,128]{3,2,1,0:T(8,128)}, f32[3,2,64,128]{3,2,1,0:T(8,128)}, u32[]{:S(2)}, u32[]{:S(2)}) collective-permute-start(f32[3,2,64,128]{3,2,1,0:T(8,128)} %get-tuple-element.32), channel_id=1, source_target_pairs={{2,0},{4,2},{6,4},{8,6},{10,8},{12,10},{14,12},{16,14},{18,16},{20... | collective-permute-start | bytes 589832 | tf_op jit(solution)/shard_map/ppermute | solution.py:23
  10.8 16.2 %copy-start = (f32[3,16,64,128]{3,2,1,0:T(8,128)S(1)}, f32[3,16,64,128]{3,2,1,0:T(8,128)}, u32[]{:S(2)}) copy-start(f32[3,16,64,128]{3,2,1,0:T(8,128)} %param.9) | copy-start | bytes 4718596
  10.8 88.3 %collective-permute-start.4 = (f32[3,2,64,128]{3,2,1,0:T(8,128)}, f32[3,2,64,128]{3,2,1,0:T(8,128)}, u32[]{:S(2)}, u32[]{:S(2)}) collective-permute-start(f32[3,2,64,128]{3,2,1,0:T(8,128)} %get-tuple-element.35), channel_id=1, source_target_pairs={{0,2},{2,4},{4,6},{6,8},{8,10},{10,12},{12,14},{14,16},{16,18},{18... | collective-permute-start | bytes 589832 | tf_op jit(solution)/shard_map/ppermute | solution.py:22
  12.8 87.8 %collective-permute-start.5 = (f32[3,2,64,128]{3,2,1,0:T(8,128)S(1)}, f32[3,2,64,128]{3,2,1,0:T(8,128)}, u32[]{:S(2)}, u32[]{:S(2)}) collective-permute-start(f32[3,2,64,128]{3,2,1,0:T(8,128)S(1)} %get-tuple-element.34), channel_id=1, source_target_pairs={{2,0},{4,2},{6,4},{8,6},{10,8},{12,10},{14,12},{16,14},{18,16},{20... | collective-permute-start | bytes 589832 | tf_op jit(solution)/shard_map/ppermute | solution.py:23
  25.2 1.3 copy-start.17
  33.4 44.9 %copy-start.14 = (f32[1152]{0:T(1024)S(1)}, f32[1152]{0:T(1024)}, u32[]{:S(2)}) copy-start(f32[1152]{0:T(1024)} %param.14) | copy-start | bytes 13828
  33.4 44.9 %copy-start.15 = (f32[1152]{0:T(1024)S(1)}, f32[1152]{0:T(1024)}, u32[]{:S(2)}) copy-start(f32[1152]{0:T(1024)} %param.13) | copy-start | bytes 13828
  33.4 45.3 %copy-start.2 = (f32[3,16,64,128]{3,2,1,0:T(8,128)S(1)}, f32[3,16,64,128]{3,2,1,0:T(8,128)}, u32[]{:S(2)}) copy-start(f32[3,16,64,128]{3,2,1,0:T(8,128)} %param.8) | copy-start | bytes 4718596
  78.7 2.0 %copy-start.1 = (f32[3,16,64,128]{3,2,1,0:T(8,128)S(1)}, f32[3,16,64,128]{3,2,1,0:T(8,128)}, u32[]{:S(2)}) copy-start(f32[3,16,64,128]{3,2,1,0:T(8,128)} %param.9) | copy-start | bytes 4718596
  82.4 7.2 %copy-start.8 = (f32[3,1152]{1,0:T(4,128)}, f32[3,1152]{1,0:T(4,128)S(1)}, u32[]{:S(2)}) copy-start(f32[3,1152]{1,0:T(4,128)S(1)} %pad_maximum_fusion.9) | copy-start | bytes 41476
  91.8 7.3 %copy-start.10 = (f32[3,18,64,128]{3,2,1,0:T(8,128)}, f32[3,18,64,128]{3,2,1,0:T(8,128)S(1)}, u32[]{:S(2)}) copy-start(f32[3,18,64,128]{3,2,1,0:T(8,128)S(1)} %get-tuple-element.26) | copy-start | bytes 5308420
  93.0 6.1 %copy-start.6 = (f32[3,18,64,128]{3,2,1,0:T(8,128)}, f32[3,18,64,128]{3,2,1,0:T(8,128)S(1)}, u32[]{:S(2)}) copy-start(f32[3,18,64,128]{3,2,1,0:T(8,128)S(1)} %get-tuple-element.52) | copy-start | bytes 5308420
  93.0 16.6 %copy-start.3 = (f32[3,20,64,128]{3,2,1,0:T(8,128)}, f32[3,20,64,128]{3,2,1,0:T(8,128)S(1)}, u32[]{:S(2)}) copy-start(f32[3,20,64,128]{3,2,1,0:T(8,128)S(1)} %get-tuple-element.53) | copy-start | bytes 5898244
  93.1 14.8 %collective-permute-start.2 = (f32[3,20,2,128]{3,2,1,0:T(2,128)S(1)}, f32[3,20,2,128]{3,2,1,0:T(2,128)S(1)}, u32[]{:S(2)}, u32[]{:S(2)}) collective-permute-start(f32[3,20,2,128]{3,2,1,0:T(2,128)S(1)} %get-tuple-element.13), channel_id=1, source_target_pairs={{0,1},{2,3},{4,5},{6,7},{8,9},{10,11},{12,13},{14,15},{16,17},{18,... | collective-permute-start | bytes 184328 | tf_op jit(solution)/shard_map/ppermute | solution.py:22
  94.4 13.5 %collective-permute-start.3 = (f32[3,20,2,128]{3,2,1,0:T(2,128)S(1)}, f32[3,20,2,128]{3,2,1,0:T(2,128)S(1)}, u32[]{:S(2)}, u32[]{:S(2)}) collective-permute-start(f32[3,20,2,128]{3,2,1,0:T(2,128)S(1)} %get-tuple-element.14), channel_id=1, source_target_pairs={{1,0},{3,2},{5,4},{7,6},{9,8},{11,10},{13,12},{15,14},{17,16},{19,... | collective-permute-start | bytes 184328 | tf_op jit(solution)/shard_map/ppermute | solution.py:23
  100.7 13.7 %copy-start.11 = (f32[3,18,64,128]{3,2,1,0:T(8,128)}, f32[3,18,64,128]{3,2,1,0:T(8,128)S(1)}, u32[]{:S(2)}) copy-start(f32[3,18,64,128]{3,2,1,0:T(8,128)S(1)} %get-tuple-element.29) | copy-start | bytes 5308420
  101.9 7.7 %copy-start.7 = (f32[3,18,64,128]{3,2,1,0:T(8,128)}, f32[3,18,64,128]{3,2,1,0:T(8,128)S(1)}, u32[]{:S(2)}) copy-start(f32[3,18,64,128]{3,2,1,0:T(8,128)S(1)} %get-tuple-element.56) | copy-start | bytes 5308420
  101.9 8.9 %copy-start.4 = (f32[3,20,64,128]{3,2,1,0:T(8,128)}, f32[3,20,64,128]{3,2,1,0:T(8,128)S(1)}, u32[]{:S(2)}) copy-start(f32[3,20,64,128]{3,2,1,0:T(8,128)S(1)} %get-tuple-element.57) | copy-start | bytes 5898244
  102.0 8.8 %collective-permute-start.6 = (f32[3,20,2,128]{3,2,1,0:T(2,128)S(1)}, f32[3,20,2,128]{3,2,1,0:T(2,128)S(1)}, u32[]{:S(2)}, u32[]{:S(2)}) collective-permute-start(f32[3,20,2,128]{3,2,1,0:T(2,128)S(1)} %get-tuple-element.15), channel_id=1, source_target_pairs={{0,1},{2,3},{4,5},{6,7},{8,9},{10,11},{12,13},{14,15},{16,17},{18,... | collective-permute-start | bytes 184328 | tf_op jit(solution)/shard_map/ppermute | solution.py:22
  103.3 7.5 %collective-permute-start.7 = (f32[3,20,2,128]{3,2,1,0:T(2,128)S(1)}, f32[3,20,2,128]{3,2,1,0:T(2,128)S(1)}, u32[]{:S(2)}, u32[]{:S(2)}) collective-permute-start(f32[3,20,2,128]{3,2,1,0:T(2,128)S(1)} %get-tuple-element.16), channel_id=1, source_target_pairs={{1,0},{3,2},{5,4},{7,6},{9,8},{11,10},{13,12},{15,14},{17,16},{19,... | collective-permute-start | bytes 184328 | tf_op jit(solution)/shard_map/ppermute | solution.py:23
  110.8 3.6 %copy-start.9 = (f32[192,16,3]{0,1,2:T(8,128)S(1)}, f32[192,16,3]{0,1,2:T(8,128)}, u32[]{:S(2)}) copy-start(f32[192,16,3]{0,1,2:T(8,128)} %broadcast_multiply_fusion) | copy-start | bytes 110596
  110.8 3.6 %copy-start.18 = (s32[192]{0:T(256)S(1)}, s32[192]{0:T(256)}, u32[]{:S(2)}) copy-start(s32[192]{0:T(256)} %copy-done.17) | copy-start | bytes 2308
  110.8 3.6 %copy-start.20 = (f32[192]{0:T(256)S(1)}, f32[192]{0:T(256)}, u32[]{:S(2)}) copy-start(f32[192]{0:T(256)} %copy-done.19) | copy-start | bytes 2308
  114.4 20.4 %copy-start.5 = (f32[16,64,128]{2,1,0:T(8,128)S(1)}, f32[16,64,128]{2,1,0:T(8,128)}, u32[]{:S(2)}) copy-start(f32[16,64,128]{2,1,0:T(8,128)} %get-tuple-element.21) | copy-start | bytes 1572868
  141.2 7.1 %collective-permute-start.8 = (f32[3,2,64,128]{3,2,1,0:T(8,128)S(1)}, f32[3,2,64,128]{3,2,1,0:T(8,128)S(1)}, u32[]{:S(2)}, u32[]{:S(2)}) collective-permute-start(f32[3,2,64,128]{3,2,1,0:T(8,128)S(1)} %get-tuple-element.19), channel_id=1, source_target_pairs={{2,0},{4,2},{6,4},{8,6},{10,8},{12,10},{14,12},{16,14},{18,16},{20... | collective-permute-start | bytes 589832 | tf_op jit(solution)/shard_map/ppermute | solution.py:23
  143.1 7.9 %collective-permute-start.9 = (f32[3,2,64,128]{3,2,1,0:T(8,128)S(1)}, f32[3,2,64,128]{3,2,1,0:T(8,128)S(1)}, u32[]{:S(2)}, u32[]{:S(2)}) collective-permute-start(f32[3,2,64,128]{3,2,1,0:T(8,128)S(1)} %get-tuple-element.20), channel_id=1, source_target_pairs={{0,2},{2,4},{4,6},{6,8},{8,10},{10,12},{12,14},{14,16},{16,18},{18... | collective-permute-start | bytes 589832 | tf_op jit(solution)/shard_map/ppermute | solution.py:22
  152.4 6.1 %collective-permute-start.10 = (f32[3,16,2,128]{3,2,1,0:T(2,128)S(1)}, f32[3,16,2,128]{3,2,1,0:T(2,128)S(1)}, u32[]{:S(2)}, u32[]{:S(2)}) collective-permute-start(f32[3,16,2,128]{3,2,1,0:T(2,128)S(1)} %get-tuple-element.17), channel_id=1, source_target_pairs={{1,0},{3,2},{5,4},{7,6},{9,8},{11,10},{13,12},{15,14},{17,16},{19,... | collective-permute-start | bytes 147464 | tf_op jit(solution)/shard_map/ppermute | solution.py:23
  155.5 6.0 %collective-permute-start.11 = (f32[3,16,2,128]{3,2,1,0:T(2,128)S(1)}, f32[3,16,2,128]{3,2,1,0:T(2,128)S(1)}, u32[]{:S(2)}, u32[]{:S(2)}) collective-permute-start(f32[3,16,2,128]{3,2,1,0:T(2,128)S(1)} %get-tuple-element.18), channel_id=1, source_target_pairs={{0,1},{2,3},{4,5},{6,7},{8,9},{10,11},{12,13},{14,15},{16,17},{18,... | collective-permute-start | bytes 147464 | tf_op jit(solution)/shard_map/ppermute | solution.py:22
  (1 other events, 0.6 us)
where the time goes:
time: 164 us
  blocking collectives  40.4 us (25%)
  starting transfers between devices  33.8 us (21%)
  other arithmetic  33.1 us (20%)
  matrix products  25.8 us (16%)
  local copies, waits for them, and re-layouts  22.7 us (14%)
  waiting for transfers between devices  5.74 us (4%)
  between operations  1.99 us (1%)
    psum x1, blocking collectives, on_device(): point_velocity = lax.psum(partial_velocity, ('gy', 'gz'))  40.4 us
    ppermute x6, starting transfers between devices, with_halo(): after = lax.ppermute(initial, axis, down)  23.4 us
    dot_general x1, matrix products, on_device(): jnp.dot(spread.reshape(-1, spread.shape[3]), table_x.T, precision=highest...  20.4 us
    ppermute x6, starting transfers between devices, with_halo(): before = lax.ppermute(last, axis, up)  10.4 us
    add x3, other arithmetic, remesh_padded(): total = total + remesh_kernel(offset - moved)[None] * part  9.8 us
    select_n x4, other arithmetic, remesh_kernel(): return jnp.where(mag < 1.0, inner, jnp.where(mag < 2.0, outer, 0.0))  7.58 us
    unnamed x47, local copies, waits for them, and re-layouts  6.02 us
    ppermute x6, waiting for transfers between devices, with_halo(): before = lax.ppermute(last, axis, up)  5.72 us
  transfers between devices with their start and end apart: 12, of which 2 were waited for; matrix products, arithmetic and copies ran while one was open for 27% of the time, Pallas kernels for 0%

commit v1 on v0

--- a/solution.py
+++ b/solution.py
@@ -173,7 +173,7 @@
     partial_velocity = jnp.dot(
         compact, selector, precision=highest, preferred_element_type=jnp.float32
     )
-    point_velocity = lax.psum(partial_velocity, ("gy", "gz"))
+    point_velocity = jnp.sum(lax.all_gather(partial_velocity, ("gy", "gz")), axis=0)
     sources = blade_forces(point_velocity, chord, twist, angle_step)
     local_sources = sources[:, picked]
     spread = jnp.einsum("cq,yq,zq->cyzq", local_sources, table_y, table_z, precision=highest)

time: 164 us -> 189 us (1.15)
  the two profiles are of different devices: /device:TPU:10 before, /device:TPU:6 now
where the time goes in v1:
time: 189 us; the launch traced here: 188 us
  blocking collectives  59.8 us (32%)
  starting transfers between devices  36.9 us (20%)
  other arithmetic  33.3 us (18%)
  matrix products  25.8 us (14%)
  local copies, waits for them, and re-layouts  22.7 us (12%)
  waiting for transfers between devices  7.84 us (4%)
  between operations  1.99 us (1%)
    all_gather x1, blocking collectives, on_device(): lax.all_gather(partial_velocity, ('gy', 'gz'))  59.8 us
    ppermute x6, starting transfers between devices, with_halo(): after = lax.ppermute(initial, axis, down)  27 us
    dot_general x1, matrix products, on_device(): jnp.dot(spread.reshape(-1, spread.shape[3]), table_x.T, precision=highest...  20.4 us
    ppermute x6, starting transfers between devices, with_halo(): before = lax.ppermute(last, axis, up)  9.88 us
    add x3, other arithmetic, remesh_padded(): total = total + remesh_kernel(offset - moved)[None] * part  9.8 us
    ppermute x6, waiting for transfers between devices, with_halo(): before = lax.ppermute(last, axis, up)  7.83 us
    select_n x4, other arithmetic, remesh_kernel(): return jnp.where(mag < 1.0, inner, jnp.where(mag < 2.0, outer, 0.0))  7.58 us
    unnamed x47, local copies, waits for them, and re-layouts  6.02 us
  transfers between devices with their start and end apart: 12, of which 2 were waited for; matrix products, arithmetic and copies ran while one was open for 24% of the time, Pallas kernels for 0%

profile of v1, /device:TPU:6, one launch (start us, length us, event | category | flops | bytes accessed | tf_op | source)
XLA Modules:
  0.0 188.3 jit_solution(11001651823822679618)
XLA Ops:
  0.6 1.8 fusion.251
  2.5 2.0 %collective-permute-start = (f32[3,2,64,128]{3,2,1,0:T(8,128)}, f32[3,2,64,128]{3,2,1,0:T(8,128)}, u32[]{:S(2)}, u32[]{:S(2)}) collective-permute-start(f32[3,2,64,128]{3,2,1,0:T(8,128)} %get-tuple-element.37), channel_id=1, source_target_pairs={{0,2},{2,4},{4,6},{6,8},{8,10},{10,12},{12,14},{14,16},{16,18},{18... | collective-permute-start | bytes 589832 | tf_op jit(solution)/shard_map/ppermute | solution.py:22
  4.5 3.6 %collective-permute-start.1 = (f32[3,2,64,128]{3,2,1,0:T(8,128)}, f32[3,2,64,128]{3,2,1,0:T(8,128)}, u32[]{:S(2)}, u32[]{:S(2)}) collective-permute-start(f32[3,2,64,128]{3,2,1,0:T(8,128)} %get-tuple-element.36), channel_id=1, source_target_pairs={{2,0},{4,2},{6,4},{8,6},{10,8},{12,10},{14,12},{16,14},{18,16},{20... | collective-permute-start | bytes 589832 | tf_op jit(solution)/shard_map/ppermute | solution.py:23
  8.2 1.7 fusion.252
  9.9 2.0 %collective-permute-start.4 = (f32[3,2,64,128]{3,2,1,0:T(8,128)}, f32[3,2,64,128]{3,2,1,0:T(8,128)}, u32[]{:S(2)}, u32[]{:S(2)}) collective-permute-start(f32[3,2,64,128]{3,2,1,0:T(8,128)} %get-tuple-element.39), channel_id=1, source_target_pairs={{0,2},{2,4},{4,6},{6,8},{8,10},{10,12},{12,14},{14,16},{16,18},{18... | collective-permute-start | bytes 589832 | tf_op jit(solution)/shard_map/ppermute | solution.py:22
  11.9 3.6 %collective-permute-start.5 = (f32[3,2,64,128]{3,2,1,0:T(8,128)S(1)}, f32[3,2,64,128]{3,2,1,0:T(8,128)}, u32[]{:S(2)}, u32[]{:S(2)}) collective-permute-start(f32[3,2,64,128]{3,2,1,0:T(8,128)S(1)} %get-tuple-element.38), channel_id=1, source_target_pairs={{2,0},{4,2},{6,4},{8,6},{10,8},{12,10},{14,12},{16,14},{18,16},{20... | collective-permute-start | bytes 589832 | tf_op jit(solution)/shard_map/ppermute | solution.py:23
  15.6 5.0 %sort.17 = (s32[1152]{0:T(1024)}, s32[1152]{0:T(1024)S(1)}) sort(s32[1152]{0:T(1024)S(1)} %get-tuple-element.67, s32[1152]{0:T(1024)S(1)} %iota.43), dimensions={0}, to_apply=%region_0.1 | sort | flops 12672 | bytes 18432 | tf_op jit(solution)/shard_map/jit(argsort)/sort | solution.py:152
  20.7 1.4 gather_fusion.3
  25.2 3.6 %convolution_bitcast_fusion = f32[3072,192]{0,1:T(8,128)} fusion(f32[3072,128]{1,0:T(8,128)S(1)} %bitcast.51, f32[192]{0:T(256)S(1)} %get-tuple-element.12, s32[192]{0:T(256)S(1)} %get-tuple-element.9), kind=kOutput, calls=%fused_computation.18 | convolution fusion | flops 906461184 | bytes 3933696 | tf_op jit(solution)/shard_map/dot_general | solution.py:165
  28.8 2.2 %copy.37 = f32[3072,192]{1,0:T(8,128)S(1)} copy(f32[3072,192]{0,1:T(8,128)} %convolution_bitcast_fusion) | data formatting | bytes 4718592
  31.9 1.4 gather_fusion
  33.5 1.4 fusion.254
  35.4 59.8 %all-gather.1 = f32[32,3,1152]{2,1,0:T(4,128)S(1)} all-gather(f32[1,3,1152]{2,1,0:T(4,128)S(1)} %convolution_bitcast_fusion.1), channel_id=2, replica_groups=mesh['gy'=16,'gz'=2] {'gy','gz'}, dimensions={0}, use_global_device_ids=true | all-gather | bytes 456192 | tf_op jit(solution)/shard_map/all_gather | solution.py:176
  98.4 1.3 fusion.103
  101.2 1.7 gather_fusion.4
  103.0 4.3 %fusion.92 = (f32[16,64,128]{2,1,0:T(8,128)}, f32[16,64,128]{2,1,0:T(8,128)}, f32[16,64,128]{2,1,0:T(8,128)}, f32[16,64,128]{2,1,0:T(8,128)}) fusion(f32[16,64,128]{2,1,0:T(8,128)} %get-tuple-element.26), kind=kLoop, calls=%fused_computation.199 | loop fusion | flops 9437184 | bytes 2621440 | tf_op jit(solution)/shard_map/jit(_where)/select_n | solution.py:32
  110.8 1.3 collective-permute-start.2
  112.1 6.5 %collective-permute-start.3 = (f32[3,20,2,128]{3,2,1,0:T(2,128)S(1)}, f32[3,20,2,128]{3,2,1,0:T(2,128)S(1)}, u32[]{:S(2)}, u32[]{:S(2)}) collective-permute-start(f32[3,20,2,128]{3,2,1,0:T(2,128)S(1)} %get-tuple-element.18), channel_id=1, source_target_pairs={{1,0},{3,2},{5,4},{7,6},{9,8},{11,10},{13,12},{15,14},{17,16},{19,... | collective-permute-start | bytes 184328 | tf_op jit(solution)/shard_map/ppermute | solution.py:23
  122.8 4.7 %collective-permute-start.7 = (f32[3,20,2,128]{3,2,1,0:T(2,128)S(1)}, f32[3,20,2,128]{3,2,1,0:T(2,128)S(1)}, u32[]{:S(2)}, u32[]{:S(2)}) collective-permute-start(f32[3,20,2,128]{3,2,1,0:T(2,128)S(1)} %get-tuple-element.20), channel_id=1, source_target_pairs={{1,0},{3,2},{5,4},{7,6},{9,8},{11,10},{13,12},{15,14},{17,16},{19,... | collective-permute-start | bytes 184328 | tf_op jit(solution)/shard_map/ppermute | solution.py:23
  127.5 1.7 pad_maximum_fusion
  130.5 3.5 %select_maximum_fusion = f32[3,20,68,132]{3,2,1,0:T(8,128)} fusion(f32[3,20,2,128]{3,2,1,0:T(2,128)S(1)} %collective-permute-done.7, f32[3,20,64,128]{3,2,1,0:T(8,128)S(1)} %get-tuple-element.61, f32[3,20,2,128]{3,2,1,0:T(2,128)S(1)} %collective-permute-done.6), kind=kLoop, calls=%fused_computation.15 | loop fusion | flops 4308480 | bytes 4243200 | tf_op jit(solution)/shard_map/concatenate | solution.py:24
  134.1 20.4 %fusion.30 = f32[3,16,64,128]{3,2,1,0:T(8,128)} fusion(f32[3,16,64,128]{3,2,1,0:T(8,128)S(1)} %copy-done.2, f32[3,20,64,128]{3,2,1,0:T(8,128)} %copy-done.4, f32[3,20,2,128]{3,2,1,0:T(2,128)S(1)} %collective-permute-done.7, f32[3,20,2,128]{3,2,1,0:T(2,128)S(1)} %collective-permute-done.6, f32[3,20,64,128]{3,2,1,0:T(8,128)} %copy-done.3, ...), kind=kOutput, calls=%fused_computation.71 | convolution fusion | flops 929464320 | bytes 29947392 | tf_op jit(solution)/shard_map/dot_general | solution.py:180
  154.4 6.4 %fusion.48 = f32[3,16,64,128]{3,2,1,0:T(8,128)S(1)} fusion(f32[3,16,64,128]{3,2,1,0:T(8,128)} %fusion.30, f32[16,64,128]{2,1,0:T(8,128)} %get-tuple-element.53, f32[16,64,128]{2,1,0:T(8,128)} %get-tuple-element.52, f32[16,64,128]{2,1,0:T(8,128)S(1)} %copy-done.5, f32[16,64,128]{2,1,0:T(8,128)} %get-tuple-element.51, f32[16,64,128]{2,1,0:T(8,128)} %get-tuple-element.50), kind=kLoop, calls=%fused_computation.89 | loop fusion | flops 3538944 | bytes 5767168 | tf_op jit(solution)/shard_map/add | solution.py:73
  160.9 5.6 %collective-permute-start.8 = (f32[3,2,64,128]{3,2,1,0:T(8,128)S(1)}, f32[3,2,64,128]{3,2,1,0:T(8,128)S(1)}, u32[]{:S(2)}, u32[]{:S(2)}) collective-permute-start(f32[3,2,64,128]{3,2,1,0:T(8,128)S(1)} %get-tuple-element.23), channel_id=1, source_target_pairs={{2,0},{4,2},{6,4},{8,6},{10,8},{12,10},{14,12},{16,14},{18,16},{20... | collective-permute-start | bytes 589832 | tf_op jit(solution)/shard_map/ppermute | solution.py:23
  166.5 1.9 %collective-permute-start.9 = (f32[3,2,64,128]{3,2,1,0:T(8,128)S(1)}, f32[3,2,64,128]{3,2,1,0:T(8,128)S(1)}, u32[]{:S(2)}, u32[]{:S(2)}) collective-permute-start(f32[3,2,64,128]{3,2,1,0:T(8,128)S(1)} %get-tuple-element.24), channel_id=1, source_target_pairs={{0,2},{2,4},{4,6},{6,8},{8,10},{10,12},{12,14},{14,16},{16,18},{18... | collective-permute-start | bytes 589832 | tf_op jit(solution)/shard_map/ppermute | solution.py:22
  168.5 1.5 fusion.87
  171.2 4.8 %collective-permute-done.9 = f32[3,2,64,128]{3,2,1,0:T(8,128)S(1)} collective-permute-done((f32[3,2,64,128]{3,2,1,0:T(8,128)S(1)}, f32[3,2,64,128]{3,2,1,0:T(8,128)S(1)}, u32[]{:S(2)}, u32[]{:S(2)}) %collective-permute-start.9) | collective-permute-done | bytes 196640 | tf_op jit(solution)/shard_map/ppermute | solution.py:22
  176.0 1.3 fusion.15
  177.3 2.9 %collective-permute-start.10 = (f32[3,16,2,128]{3,2,1,0:T(2,128)S(1)}, f32[3,16,2,128]{3,2,1,0:T(2,128)S(1)}, u32[]{:S(2)}, u32[]{:S(2)}) collective-permute-start(f32[3,16,2,128]{3,2,1,0:T(2,128)S(1)} %get-tuple-element.21), channel_id=1, source_target_pairs={{1,0},{3,2},{5,4},{7,6},{9,8},{11,10},{13,12},{15,14},{17,16},{19,... | collective-permute-start | bytes 147464 | tf_op jit(solution)/shard_map/ppermute | solution.py:23
  181.6 1.7 fusion.82
  183.2 3.0 %collective-permute-done.11 = f32[3,16,2,128]{3,2,1,0:T(2,128)S(1)} collective-permute-done((f32[3,16,2,128]{3,2,1,0:T(2,128)S(1)}, f32[3,16,2,128]{3,2,1,0:T(2,128)S(1)}, u32[]{:S(2)}, u32[]{:S(2)}) %collective-permute-start.11) | collective-permute-done | bytes 49184 | tf_op jit(solution)/shard_map/ppermute | solution.py:22
  186.3 2.1 %fusion.7 = f32[3,16,64,128]{3,2,1,0:T(8,128)} fusion(f32[3,16,2,128]{3,2,1,0:T(2,128)S(1)} %collective-permute-done.11, f32[3,16,64,128]{3,2,1,0:T(8,128)S(1)} %fusion.15, f32[3,16,2,128]{3,2,1,0:T(2,128)S(1)} %collective-permute-done.10, f32[16,64,128]{2,1,0:T(8,128)S(1)} %get-tuple-element.46, f32[16,64,128]{2,1,0:T(8,128)S(1)} %get-tuple-element.47, ...), kind=kLoop, calls=%fused_computation.48 | loop fusion | flops 5111808 | bytes 5865472 | tf_op jit(solution)/shard_map/add | solution.py:73
  (103 shorter events, 19.7 us)
Async XLA Ops:
  0.6 15.0 %copy-start.16 = (s32[1152]{0:T(1024)S(1)}, s32[1152]{0:T(1024)}, u32[]{:S(2)}) copy-start(s32[1152]{0:T(1024)} %param.10) | copy-start | bytes 13828
  0.6 21.5 %copy-start.12 = (s32[3,1152]{1,0:T(4,128)S(1)}, s32[3,1152]{1,0:T(4,128)}, u32[]{:S(2)}) copy-start(s32[3,1152]{1,0:T(4,128)} %param.11) | copy-start | bytes 41476
  2.5 21.0 %copy-start.13 = (f32[3,1152]{1,0:T(4,128)S(1)}, f32[3,1152]{1,0:T(4,128)}, u32[]{:S(2)}) copy-start(f32[3,1152]{1,0:T(4,128)} %param.12) | copy-start | bytes 41476
  2.5 105.5 %collective-permute-start = (f32[3,2,64,128]{3,2,1,0:T(8,128)}, f32[3,2,64,128]{3,2,1,0:T(8,128)}, u32[]{:S(2)}, u32[]{:S(2)}) collective-permute-start(f32[3,2,64,128]{3,2,1,0:T(8,128)} %get-tuple-element.37), channel_id=1, source_target_pairs={{0,2},{2,4},{4,6},{6,8},{8,10},{10,12},{12,14},{14,16},{16,18},{18... | collective-permute-start | bytes 589832 | tf_op jit(solution)/shard_map/ppermute | solution.py:22
  4.5 105.0 %collective-permute-start.1 = (f32[3,2,64,128]{3,2,1,0:T(8,128)}, f32[3,2,64,128]{3,2,1,0:T(8,128)}, u32[]{:S(2)}, u32[]{:S(2)}) collective-permute-start(f32[3,2,64,128]{3,2,1,0:T(8,128)} %get-tuple-element.36), channel_id=1, source_target_pairs={{2,0},{4,2},{6,4},{8,6},{10,8},{12,10},{14,12},{16,14},{18,16},{20... | collective-permute-start | bytes 589832 | tf_op jit(solution)/shard_map/ppermute | solution.py:23
  9.9 15.3 %copy-start = (f32[3,16,64,128]{3,2,1,0:T(8,128)S(1)}, f32[3,16,64,128]{3,2,1,0:T(8,128)}, u32[]{:S(2)}) copy-start(f32[3,16,64,128]{3,2,1,0:T(8,128)} %param.9) | copy-start | bytes 4718596
  9.9 108.7 %collective-permute-start.4 = (f32[3,2,64,128]{3,2,1,0:T(8,128)}, f32[3,2,64,128]{3,2,1,0:T(8,128)}, u32[]{:S(2)}, u32[]{:S(2)}) collective-permute-start(f32[3,2,64,128]{3,2,1,0:T(8,128)} %get-tuple-element.39), channel_id=1, source_target_pairs={{0,2},{2,4},{4,6},{6,8},{8,10},{10,12},{12,14},{14,16},{16,18},{18... | collective-permute-start | bytes 589832 | tf_op jit(solution)/shard_map/ppermute | solution.py:22
  11.9 108.3 %collective-permute-start.5 = (f32[3,2,64,128]{3,2,1,0:T(8,128)S(1)}, f32[3,2,64,128]{3,2,1,0:T(8,128)}, u32[]{:S(2)}, u32[]{:S(2)}) collective-permute-start(f32[3,2,64,128]{3,2,1,0:T(8,128)S(1)} %get-tuple-element.38), channel_id=1, source_target_pairs={{2,0},{4,2},{6,4},{8,6},{10,8},{12,10},{14,12},{16,14},{18,16},{20... | collective-permute-start | bytes 589832 | tf_op jit(solution)/shard_map/ppermute | solution.py:23
  23.4 1.3 copy-start.17
  31.8 64.2 %copy-start.14 = (f32[1152]{0:T(1024)S(1)}, f32[1152]{0:T(1024)}, u32[]{:S(2)}) copy-start(f32[1152]{0:T(1024)} %param.14) | copy-start | bytes 13828
  31.8 64.2 %copy-start.15 = (f32[1152]{0:T(1024)S(1)}, f32[1152]{0:T(1024)}, u32[]{:S(2)}) copy-start(f32[1152]{0:T(1024)} %param.13) | copy-start | bytes 13828
  31.8 64.6 %copy-start.2 = (f32[3,16,64,128]{3,2,1,0:T(8,128)S(1)}, f32[3,16,64,128]{3,2,1,0:T(8,128)}, u32[]{:S(2)}) copy-start(f32[3,16,64,128]{3,2,1,0:T(8,128)} %param.8) | copy-start | bytes 4718596
  96.4 2.0 %copy-start.1 = (f32[3,16,64,128]{3,2,1,0:T(8,128)S(1)}, f32[3,16,64,128]{3,2,1,0:T(8,128)}, u32[]{:S(2)}) copy-start(f32[3,16,64,128]{3,2,1,0:T(8,128)} %param.9) | copy-start | bytes 4718596
  100.1 7.2 %copy-start.8 = (f32[3,1152]{1,0:T(4,128)}, f32[3,1152]{1,0:T(4,128)S(1)}, u32[]{:S(2)}) copy-start(f32[3,1152]{1,0:T(4,128)S(1)} %pad_maximum_fusion.9) | copy-start | bytes 41476
  109.5 9.1 %copy-start.10 = (f32[3,18,64,128]{3,2,1,0:T(8,128)}, f32[3,18,64,128]{3,2,1,0:T(8,128)S(1)}, u32[]{:S(2)}) copy-start(f32[3,18,64,128]{3,2,1,0:T(8,128)S(1)} %get-tuple-element.30) | copy-start | bytes 5308420
  110.7 7.9 %copy-start.6 = (f32[3,18,64,128]{3,2,1,0:T(8,128)}, f32[3,18,64,128]{3,2,1,0:T(8,128)S(1)}, u32[]{:S(2)}) copy-start(f32[3,18,64,128]{3,2,1,0:T(8,128)S(1)} %get-tuple-element.56) | copy-start | bytes 5308420
  110.7 18.6 %copy-start.3 = (f32[3,20,64,128]{3,2,1,0:T(8,128)}, f32[3,20,64,128]{3,2,1,0:T(8,128)S(1)}, u32[]{:S(2)}) copy-start(f32[3,20,64,128]{3,2,1,0:T(8,128)S(1)} %get-tuple-element.57) | copy-start | bytes 5898244
  110.8 16.7 %collective-permute-start.2 = (f32[3,20,2,128]{3,2,1,0:T(2,128)S(1)}, f32[3,20,2,128]{3,2,1,0:T(2,128)S(1)}, u32[]{:S(2)}, u32[]{:S(2)}) collective-permute-start(f32[3,20,2,128]{3,2,1,0:T(2,128)S(1)} %get-tuple-element.17), channel_id=1, source_target_pairs={{0,1},{2,3},{4,5},{6,7},{8,9},{10,11},{12,13},{14,15},{16,17},{18,... | collective-permute-start | bytes 184328 | tf_op jit(solution)/shard_map/ppermute | solution.py:22
  112.1 15.4 %collective-permute-start.3 = (f32[3,20,2,128]{3,2,1,0:T(2,128)S(1)}, f32[3,20,2,128]{3,2,1,0:T(2,128)S(1)}, u32[]{:S(2)}, u32[]{:S(2)}) collective-permute-start(f32[3,20,2,128]{3,2,1,0:T(2,128)S(1)} %get-tuple-element.18), channel_id=1, source_target_pairs={{1,0},{3,2},{5,4},{7,6},{9,8},{11,10},{13,12},{15,14},{17,16},{19,... | collective-permute-start | bytes 184328 | tf_op jit(solution)/shard_map/ppermute | solution.py:23
  120.2 13.9 %copy-start.11 = (f32[3,18,64,128]{3,2,1,0:T(8,128)}, f32[3,18,64,128]{3,2,1,0:T(8,128)S(1)}, u32[]{:S(2)}) copy-start(f32[3,18,64,128]{3,2,1,0:T(8,128)S(1)} %get-tuple-element.33) | copy-start | bytes 5308420
  121.4 7.9 %copy-start.7 = (f32[3,18,64,128]{3,2,1,0:T(8,128)}, f32[3,18,64,128]{3,2,1,0:T(8,128)S(1)}, u32[]{:S(2)}) copy-start(f32[3,18,64,128]{3,2,1,0:T(8,128)S(1)} %get-tuple-element.60) | copy-start | bytes 5308420
  121.4 9.1 %copy-start.4 = (f32[3,20,64,128]{3,2,1,0:T(8,128)}, f32[3,20,64,128]{3,2,1,0:T(8,128)S(1)}, u32[]{:S(2)}) copy-start(f32[3,20,64,128]{3,2,1,0:T(8,128)S(1)} %get-tuple-element.61) | copy-start | bytes 5898244
  121.5 9.0 %collective-permute-start.6 = (f32[3,20,2,128]{3,2,1,0:T(2,128)S(1)}, f32[3,20,2,128]{3,2,1,0:T(2,128)S(1)}, u32[]{:S(2)}, u32[]{:S(2)}) collective-permute-start(f32[3,20,2,128]{3,2,1,0:T(2,128)S(1)} %get-tuple-element.19), channel_id=1, source_target_pairs={{0,1},{2,3},{4,5},{6,7},{8,9},{10,11},{12,13},{14,15},{16,17},{18,... | collective-permute-start | bytes 184328 | tf_op jit(solution)/shard_map/ppermute | solution.py:22
  122.8 7.7 %collective-permute-start.7 = (f32[3,20,2,128]{3,2,1,0:T(2,128)S(1)}, f32[3,20,2,128]{3,2,1,0:T(2,128)S(1)}, u32[]{:S(2)}, u32[]{:S(2)}) collective-permute-start(f32[3,20,2,128]{3,2,1,0:T(2,128)S(1)} %get-tuple-element.20), channel_id=1, source_target_pairs={{1,0},{3,2},{5,4},{7,6},{9,8},{11,10},{13,12},{15,14},{17,16},{19,... | collective-permute-start | bytes 184328 | tf_op jit(solution)/shard_map/ppermute | solution.py:23
  130.5 3.6 %copy-start.9 = (f32[192,16,3]{0,1,2:T(8,128)S(1)}, f32[192,16,3]{0,1,2:T(8,128)}, u32[]{:S(2)}) copy-start(f32[192,16,3]{0,1,2:T(8,128)} %broadcast_multiply_fusion) | copy-start | bytes 110596
  130.5 3.6 %copy-start.18 = (s32[192]{0:T(256)S(1)}, s32[192]{0:T(256)}, u32[]{:S(2)}) copy-start(s32[192]{0:T(256)} %copy-done.17) | copy-start | bytes 2308
  130.5 3.6 %copy-start.20 = (f32[192]{0:T(256)S(1)}, f32[192]{0:T(256)}, u32[]{:S(2)}) copy-start(f32[192]{0:T(256)} %copy-done.19) | copy-start | bytes 2308
  134.1 20.4 %copy-start.5 = (f32[16,64,128]{2,1,0:T(8,128)S(1)}, f32[16,64,128]{2,1,0:T(8,128)}, u32[]{:S(2)}) copy-start(f32[16,64,128]{2,1,0:T(8,128)} %get-tuple-element.25) | copy-start | bytes 1572868
  160.9 10.3 %collective-permute-start.8 = (f32[3,2,64,128]{3,2,1,0:T(8,128)S(1)}, f32[3,2,64,128]{3,2,1,0:T(8,128)S(1)}, u32[]{:S(2)}, u32[]{:S(2)}) collective-permute-start(f32[3,2,64,128]{3,2,1,0:T(8,128)S(1)} %get-tuple-element.23), channel_id=1, source_target_pairs={{2,0},{4,2},{6,4},{8,6},{10,8},{12,10},{14,12},{16,14},{18,16},{20... | collective-permute-start | bytes 589832 | tf_op jit(solution)/shard_map/ppermute | solution.py:23
  166.5 9.5 %collective-permute-start.9 = (f32[3,2,64,128]{3,2,1,0:T(8,128)S(1)}, f32[3,2,64,128]{3,2,1,0:T(8,128)S(1)}, u32[]{:S(2)}, u32[]{:S(2)}) collective-permute-start(f32[3,2,64,128]{3,2,1,0:T(8,128)S(1)} %get-tuple-element.24), channel_id=1, source_target_pairs={{0,2},{2,4},{4,6},{6,8},{8,10},{10,12},{12,14},{14,16},{16,18},{18... | collective-permute-start | bytes 589832 | tf_op jit(solution)/shard_map/ppermute | solution.py:22
  177.3 5.9 %collective-permute-start.10 = (f32[3,16,2,128]{3,2,1,0:T(2,128)S(1)}, f32[3,16,2,128]{3,2,1,0:T(2,128)S(1)}, u32[]{:S(2)}, u32[]{:S(2)}) collective-permute-start(f32[3,16,2,128]{3,2,1,0:T(2,128)S(1)} %get-tuple-element.21), channel_id=1, source_target_pairs={{1,0},{3,2},{5,4},{7,6},{9,8},{11,10},{13,12},{15,14},{17,16},{19,... | collective-permute-start | bytes 147464 | tf_op jit(solution)/shard_map/ppermute | solution.py:23
  180.3 6.0 %collective-permute-start.11 = (f32[3,16,2,128]{3,2,1,0:T(2,128)S(1)}, f32[3,16,2,128]{3,2,1,0:T(2,128)S(1)}, u32[]{:S(2)}, u32[]{:S(2)}) collective-permute-start(f32[3,16,2,128]{3,2,1,0:T(2,128)S(1)} %get-tuple-element.22), channel_id=1, source_target_pairs={{0,1},{2,3},{4,5},{6,7},{8,9},{10,11},{12,13},{14,15},{16,17},{18,... | collective-permute-start | bytes 147464 | tf_op jit(solution)/shard_map/ppermute | solution.py:22
  (1 other events, 0.6 us)
